TPU v7x, 32 devices: a whole 2x2x4 slice. The times are simulated.
32 devices in a mesh: aa: 4 (over z), ba: 8 (over y, x, core).
Axes of the slice: x: 2, y: 2, z: 4, core: 2. Of those that a mesh axis runs over, the one named last changes fastest.
Arguments:
- grad_out: bfloat16 [4096, 4096], P('aa', 'ba')
- saved_input: bfloat16 [4096, 4096], P(('aa', 'ba'))
- keep_bits: int32 [4096, 128], P(('aa', 'ba')), may hold values from -2147483648 to 2147483647, as said below
- gain: float32 [4096], replicated, may hold values from 0.5 to 1.5
Outputs:
- grad_in: bfloat16 [4096, 4096], P(('aa', 'ba'))
- gain_grad: float32 [4096], P('ba')
Inputs may be any that keep to these rules, and one draw needn't show every extreme that they name: `keep_bits`: bit k of word w in row t (bit 31 being the sign bit) is the keep flag of feature 32 * w + k of token t; about nine in ten flags are 1.
All inputs are finite; a program needn't handle non-finite values.
Results may differ from a plain program's by a relative error of at most 0.001.
Values may be sent and summed in bfloat16 or wider, within the bound.
A program may use at most 64 MiB of HBM per device.

v0:
```python
import math
import jax
import jax.numpy as jnp
from jax import lax
from jax.sharding import PartitionSpec as P

KEEP_RATE = 0.9
EPSILON = 1e-06


def unpack_bits(words):
    shifts = jnp.arange(32, dtype=jnp.int32)
    bits = jnp.right_shift(words[:, :, None], shifts[None, None, :]) & 1
    return bits.reshape(words.shape[0], words.shape[1] * 32).astype(jnp.float32)


def rows_backward(grad_rows, input_rows, word_rows, gain):
    keep = unpack_bits(word_rows)
    dropped = input_rows.astype(jnp.float32) * keep * (1.0 / KEEP_RATE)
    inverse = lax.rsqrt(jnp.mean(dropped * dropped, axis=-1, keepdims=True) + EPSILON)
    normed = dropped * inverse
    grads = grad_rows.astype(jnp.float32)
    scaled = gain[None, :] * grads
    centre = jnp.mean(scaled * normed, axis=-1, keepdims=True)
    grad_in = (inverse * (scaled - normed * centre) * keep * (1.0 / KEEP_RATE)).astype(jnp.bfloat16)
    partial_sum = jnp.sum(grads * normed, axis=0)
    return (grad_in, partial_sum)


def per_device(grad_out, saved_input, keep_bits, gain):
    groups = lax.axis_size("ba")
    rows = grad_out.shape[0] // groups
    pieces = grad_out.reshape(groups, rows, grad_out.shape[1])
    arrived = lax.all_to_all(pieces, "ba", split_axis=0, concat_axis=2, tiled=True)
    grad_rows = arrived.reshape(rows, arrived.shape[2])
    grad_in, partial_sum = rows_backward(grad_rows, saved_input, keep_bits, gain)
    total_tokens = rows * groups * lax.axis_size("aa")
    owned = lax.psum_scatter(partial_sum, "ba", scatter_dimension=0, tiled=True)
    share = lax.psum(owned, "aa")
    gain_grad = share * (1.0 / math.sqrt(total_tokens))
    return (grad_in, gain_grad)


def solution(mesh):
    placed = (P("aa", "ba"), P(("aa", "ba"), None), P(("aa", "ba"), None), P())
    return jax.shard_map(
        per_device,
        mesh=mesh,
        in_specs=placed,
        out_specs=(P(("aa", "ba"), None), P("ba")),
        check_vma=False,
    )
```

profile of v0, /device:TPU:0, one launch (start us, length us, event | category | flops | bytes accessed | tf_op | source)
XLA Modules:
  0.0 63.3 jit_solution(16669645412910738614)
XLA Ops:
  0.6 2.3 %copy.13 = bf16[8,128,512]{1,2,0:T(8,128)(2,1)} copy(bf16[8,128,512]{2,1,0:T(8,128)(2,1)} %bitcast.48) | data formatting | bytes 2097152 | tf_op jit(solution)/shard_map/reshape | solution.py:33
  2.9 0.0 copy-start
  2.9 5.3 %all-to-all-start = ((bf16[8,128,512]{1,2,0:T(8,128)(2,1)}), bf16[8,128,512]{1,2,0:T(8,128)(2,1)S(1)}, u32[]{:S(2)}, u32[]{:S(2)}) async-start(bf16[8,128,512]{1,2,0:T(8,128)(2,1)} %copy.13), calls=%async_computation | async-start | bytes 2097152 | tf_op jit(solution)/shard_map/all_to_all | solution.py:34
  8.2 0.0 copy-done
  8.2 0.0 copy-start.2
  8.2 0.0 copy-start.3
  8.3 0.7 %copy.11 = bf16[128,4096]{0,1:T(8,128)(2,1)S(1)} copy(bf16[128,4096]{1,0:T(8,128)(2,1)S(1)} %copy-done) | data formatting | bytes 2097152 | tf_op args[1]
  8.9 0.0 copy-start.1
  9.0 0.1 shift_right_arithmetic.23
  9.0 0.0 copy-done.2
  9.1 0.1 copy.12
  9.2 0.0 copy-done.3
  9.2 0.6 dynamic-slice
  10.4 0.7 %multiply_reduce_fusion = f32[128]{0:T(128)S(1)} fusion(bf16[128,4096]{0,1:T(8,128)(2,1)S(1)} %copy.11, s32[4096]{0:T(1024)S(1)} %shift_right_arithmetic.23, s32[128,128]{0,1:T(8,128)S(1)} %copy.12), kind=kLoop, calls=%fused_computation.14 | loop fusion | flops 4194176 | bytes 1131008 | tf_op jit(solution)/shard_map/reduce_sum | solution.py:20
  11.2 12.4 %all-to-all-done = bf16[8,128,512]{1,2,0:T(8,128)(2,1)S(1)} async-done(((bf16[8,128,512]{1,2,0:T(8,128)(2,1)}), bf16[8,128,512]{1,2,0:T(8,128)(2,1)S(1)}, u32[]{:S(2)}, u32[]{:S(2)}) %all-to-all-start) | async-done | bytes 1048608 | tf_op jit(solution)/shard_map/all_to_all | solution.py:34
  23.6 0.0 copy-done.1
  23.6 2.0 %fusion.7 = (f32[4096]{0:T(1024)S(1)}, f32[128]{0:T(128)S(1)}) fusion(bf16[128,4096]{0,1:T(8,128)(2,1)S(1)} %copy.11, bf16[8,128,512]{1,2,0:T(8,128)(2,1)S(1)} %all-to-all-done, f32[128]{0:T(128)S(1)} %get-tuple-element.9, s32[4096]{0:T(1024)S(1)} %shift_right_arithmetic.23, s32[128,128]{0,1:T(8,128)S(1)} %copy.12, f32[4096]{0:T(1024)S(1)} %copy-done.1), kind=kLoop, calls=%fused_computation.9 | loop fusion | flops 6287232 | bytes 2212864 | tf_op jit(solution)/shard_map/reduce_sum | solution.py:26
  25.6 1.4 %fusion.6 = bf16[128,4096]{0,1:T(8,128)(2,1)S(1)} fusion(bf16[128,4096]{0,1:T(8,128)(2,1)S(1)} %copy.11, bf16[8,128,512]{1,2,0:T(8,128)(2,1)S(1)} %all-to-all-done, f32[128]{0:T(128)S(1)} %broadcast_multiply_fusion.2, f32[128]{0:T(128)S(1)} %get-tuple-element.9, f32[4096]{0:T(1024)S(1)} %copy-done.1, f32[128]{0:T(128)S(1)} %get-tuple-element.8, ...), kind=kLoop, calls=%fused_computation.8 | loop fusion | flops 7340032 | bytes 3245568 | tf_op jit(solution)/shard_map/convert_element_type | solution.py:25
  27.1 1.3 %copy.14 = bf16[128,4096]{1,0:T(8,128)(2,1)} copy(bf16[128,4096]{0,1:T(8,128)(2,1)S(1)} %fusion.6) | data formatting | bytes 2097152
  28.4 22.3 %all-reduce = f32[4096]{0:T(1024)S(1)} all-reduce(f32[4096]{0:T(1024)S(1)} %get-tuple-element.6), channel_id=2, replica_groups=mesh['aa'=4,'ba'=8] {'ba'}, use_global_device_ids=true, to_apply=%region_3.0.clone | all-reduce | flops 4096 | bytes 32768
  50.7 0.1 dynamic-slice.1
  50.8 11.9 %psum.7 = f32[512]{0:T(512)S(1)} all-reduce(f32[512]{0:T(512)S(1)} %dynamic-slice.1), channel_id=1, replica_groups=mesh['aa'=4,'ba'=8] {'aa'}, use_global_device_ids=true, to_apply=%region_4.0 | all-reduce | flops 512 | bytes 4096 | tf_op jit(solution)/shard_map/psum | solution.py:39
  62.7 0.6 broadcast_multiply_fusion
  (3 shorter events, 0.0 us)
Async XLA Ops:
  2.9 5.3 %copy-start = (bf16[128,4096]{1,0:T(8,128)(2,1)S(1)}, bf16[128,4096]{1,0:T(8,128)(2,1)}, u32[]{:S(2)}) copy-start(bf16[128,4096]{1,0:T(8,128)(2,1)} %param.5) | copy-start | bytes 3145732
  2.9 20.7 %all-to-all-start = ((bf16[8,128,512]{1,2,0:T(8,128)(2,1)}), bf16[8,128,512]{1,2,0:T(8,128)(2,1)S(1)}, u32[]{:S(2)}, u32[]{:S(2)}) async-start(bf16[8,128,512]{1,2,0:T(8,128)(2,1)} %copy.13), calls=%async_computation | async-start | bytes 2097152 | tf_op jit(solution)/shard_map/all_to_all | solution.py:34
  8.2 0.8 %copy-start.2 = (s32[128,128]{1,0:T(8,128)S(1)}, s32[128,128]{1,0:T(8,128)}, u32[]{:S(2)}) copy-start(s32[128,128]{1,0:T(8,128)} %param.6) | copy-start | bytes 196612
  8.2 0.9 %copy-start.3 = (u32[32]{0:T(128)S(1)}, u32[32]{0:T(128)}, u32[]{:S(2)}) copy-start(u32[32]{0:T(128)} %constant.16) | copy-start | bytes 388
  8.9 14.7 %copy-start.1 = (f32[4096]{0:T(1024)S(1)}, f32[4096]{0:T(1024)}, u32[]{:S(2)}) copy-start(f32[4096]{0:T(1024)} %param.7) | copy-start | bytes 49156
where the time goes:
time: 63.6 us; the launch traced here: 63.3 us
  blocking collectives  34.2 us (54%)
  waiting for transfers between devices  12.4 us (19%)
  starting transfers between devices  5.33 us (8%)
  local copies, waits for them, and re-layouts  5.13 us (8%)
  other arithmetic  4.78 us (8%)
  between operations  1.38 us (2%)
    unnamed x1, blocking collectives  22.3 us
    all_to_all x1, waiting for transfers between devices, per_device(): lax.all_to_all(pieces, 'ba', split_axis=0, concat_axis=2, tiled=True)  12.4 us
    psum x1, blocking collectives, per_device(): share = lax.psum(owned, 'aa')  11.9 us
    all_to_all x1, starting transfers between devices, per_device(): lax.all_to_all(pieces, 'ba', split_axis=0, concat_axis=2, tiled=True)  5.33 us
    unnamed x13, local copies, waits for them, and re-layouts  2.78 us
    reshape x1, local copies, waits for them, and re-layouts, per_device(): pieces = grad_out.reshape(groups, rows, grad_out.shape[1])  2.26 us
    reduce_sum x1, other arithmetic, rows_backward(): partial_sum = jnp.sum(grads * normed, axis=0)  2.02 us
    convert_element_type x1, other arithmetic, rows_backward(): (inverse * (scaled - normed * centre) * keep * (1.0 / KEEP_RATE)).astype(...  1.43 us
  transfers between devices with their start and end apart: 1, of which 1 were waited for; matrix products, arithmetic and copies ran while one was open for 3% of the time, Pallas kernels for 0%

commit v1 on v0

--- a/solution.py
+++ b/solution.py
@@ -31,7 +31,10 @@
     groups = lax.axis_size("ba")
     rows = grad_out.shape[0] // groups
     pieces = grad_out.reshape(groups, rows, grad_out.shape[1])
-    arrived = lax.all_to_all(pieces, "ba", split_axis=0, concat_axis=2, tiled=True)
+    peers = lax.axis_size("ba")
+    shards = jnp.stack(jnp.split(pieces, peers, axis=0), axis=0)
+    shards = lax.all_to_all(shards, "ba", split_axis=0, concat_axis=0)
+    arrived = jnp.concatenate(shards, axis=2)
     grad_rows = arrived.reshape(rows, arrived.shape[2])
     grad_in, partial_sum = rows_backward(grad_rows, saved_input, keep_bits, gain)
     total_tokens = rows * groups * lax.axis_size("aa")

time: 63.6 us -> 80 us (1.26)
  local copies, waits for them, and re-layouts: 5.13 us -> 18.3 us
  other arithmetic: 4.78 us -> 7.74 us
    unnamed x13 -> x20, local copies, waits for them, and re-layouts: 2.78 us -> 14.7 us
    reshape x1 -> x0, local copies, waits for them, and re-layouts: 2.26 us -> none  [per_device(): pieces = grad_out.reshape(groups, rows, grad_out.shape[1])]
    convert_element_type x0 -> x1, local copies, waits for them, and re-layouts: none -> 1.92 us  [rows_backward(): grads = grad_rows.astype(jnp.float32)]
    convert_element_type x0 -> x1, other arithmetic: none -> 1.64 us  [rows_backward(): grads = grad_rows.astype(jnp.float32)]
    another operation x0 -> x1, local copies, waits for them, and re-layouts: none -> 1.57 us  [per_device(): shards = jnp.stack(jnp.split(pieces, peers, axis=0), axis=0)]
    convert_element_type x1, other arithmetic: 1.43 us -> 2.59 us  [rows_backward(): (inverse * (scaled - normed * centre) * keep * (1.0 / KEEP_RATE)).astype(...]
where the time goes in v1:
time: 80 us; the launch traced here: 79.5 us
  blocking collectives  34.2 us (43%)
  local copies, waits for them, and re-layouts  18.3 us (23%)
  waiting for transfers between devices  12.5 us (16%)
  other arithmetic  7.74 us (10%)
  starting transfers between devices  5.33 us (7%)
  between operations  1.39 us (2%)
    unnamed x1, blocking collectives  22.3 us
    unnamed x20, local copies, waits for them, and re-layouts  14.7 us
    all_to_all x1, waiting for transfers between devices, per_device(): shards = lax.all_to_all(shards, 'ba', split_axis=0, concat_axis=0)  12.5 us
    psum x1, blocking collectives, per_device(): share = lax.psum(owned, 'aa')  11.9 us
    all_to_all x1, starting transfers between devices, per_device(): shards = lax.all_to_all(shards, 'ba', split_axis=0, concat_axis=0)  5.33 us
    convert_element_type x1, other arithmetic, rows_backward(): (inverse * (scaled - normed * centre) * keep * (1.0 / KEEP_RATE)).astype(...  2.59 us
    reduce_sum x1, other arithmetic, rows_backward(): partial_sum = jnp.sum(grads * normed, axis=0)  2.2 us
    convert_element_type x1, local copies, waits for them, and re-layouts, rows_backward(): grads = grad_rows.astype(jnp.float32)  1.92 us
  transfers between devices with their start and end apart: 1, of which 1 were waited for; matrix products, arithmetic and copies ran while one was open for 3% of the time, Pallas kernels for 0%

profile of v1, /device:TPU:0, one launch (start us, length us, event | category | flops | bytes accessed | tf_op | source)
XLA Modules:
  0.0 79.5 jit_solution(14299120545742476879)
XLA Ops:
  0.6 0.0 copy-start
  0.6 1.7 %bitcast_dynamic-update-slice_fusion.7 = bf16[8,1,128,512]{3,2,1,0:T(8,128)(2,1)} fusion(bf16[1024,512]{1,0:T(8,128)(2,1)} %param.4), kind=kLoop, calls=%fused_computation.21 | loop fusion | bytes 262144
  2.3 1.6 %bitcast_dynamic-update-slice_fusion.6 = bf16[8,1,128,512]{3,2,1,0:T(8,128)(2,1)} fusion(bf16[8,1,128,512]{3,2,1,0:T(8,128)(2,1)} %bitcast_dynamic-update-slice_fusion.7, bf16[1024,512]{1,0:T(8,128)(2,1)} %param.4), kind=kLoop, calls=%fused_computation.20 | loop fusion | bytes 262144
  3.9 1.6 %bitcast_dynamic-update-slice_fusion.5 = bf16[8,1,128,512]{3,2,1,0:T(8,128)(2,1)} fusion(bf16[8,1,128,512]{3,2,1,0:T(8,128)(2,1)} %bitcast_dynamic-update-slice_fusion.6, bf16[1024,512]{1,0:T(8,128)(2,1)} %param.4), kind=kLoop, calls=%fused_computation.19 | loop fusion | bytes 262144
  5.4 1.6 %bitcast_dynamic-update-slice_fusion.4 = bf16[8,1,128,512]{3,2,1,0:T(8,128)(2,1)} fusion(bf16[8,1,128,512]{3,2,1,0:T(8,128)(2,1)} %bitcast_dynamic-update-slice_fusion.5, bf16[1024,512]{1,0:T(8,128)(2,1)} %param.4), kind=kLoop, calls=%fused_computation.18 | loop fusion | bytes 262144
  7.0 1.6 %bitcast_dynamic-update-slice_fusion.3 = bf16[8,1,128,512]{3,2,1,0:T(8,128)(2,1)} fusion(bf16[8,1,128,512]{3,2,1,0:T(8,128)(2,1)} %bitcast_dynamic-update-slice_fusion.4, bf16[1024,512]{1,0:T(8,128)(2,1)} %param.4), kind=kLoop, calls=%fused_computation.17 | loop fusion | bytes 262144
  8.6 1.6 %bitcast_dynamic-update-slice_fusion.2 = bf16[8,1,128,512]{3,2,1,0:T(8,128)(2,1)} fusion(bf16[8,1,128,512]{3,2,1,0:T(8,128)(2,1)} %bitcast_dynamic-update-slice_fusion.3, bf16[1024,512]{1,0:T(8,128)(2,1)} %param.4), kind=kLoop, calls=%fused_computation.16 | loop fusion | bytes 262144
  10.1 1.6 %bitcast_dynamic-update-slice_fusion.1 = bf16[8,1,128,512]{3,2,1,0:T(8,128)(2,1)} fusion(bf16[8,1,128,512]{3,2,1,0:T(8,128)(2,1)} %bitcast_dynamic-update-slice_fusion.2, bf16[1024,512]{1,0:T(8,128)(2,1)} %param.4), kind=kLoop, calls=%fused_computation.15 | loop fusion | bytes 262144
  11.7 1.6 %bitcast_dynamic-update-slice_fusion = bf16[8,1,128,512]{3,2,1,0:T(8,128)(2,1)} fusion(bf16[8,1,128,512]{3,2,1,0:T(8,128)(2,1)} %bitcast_dynamic-update-slice_fusion.1, bf16[1024,512]{1,0:T(8,128)(2,1)} %param.4), kind=kLoop, calls=%fused_computation.14 | loop fusion | bytes 262144 | tf_op jit(solution)/shard_map/stack | solution.py:35
  13.3 0.0 copy-start.2
  13.3 0.0 copy-start.3
  13.3 5.3 %all-to-all-start = ((bf16[8,1,128,512]{3,2,1,0:T(8,128)(2,1)}), bf16[8,1,128,512]{3,2,1,0:T(8,128)(2,1)S(1)}, u32[]{:S(2)}, u32[]{:S(2)}) async-start(bf16[8,1,128,512]{3,2,1,0:T(8,128)(2,1)} %bitcast_dynamic-update-slice_fusion), calls=%async_computation | async-start | bytes 2097152 | tf_op jit(solution)/shard_map/all_to_all | solution.py:36
  18.6 0.0 copy-done
  18.6 0.7 copy.11
  19.3 0.1 shift_right_arithmetic.23
  19.4 0.0 copy-done.2
  19.4 0.1 copy.12
  19.5 0.0 copy-done.3
  19.5 0.6 dynamic-slice
  20.7 0.7 multiply_reduce_fusion.1
  21.5 12.5 %all-to-all-done = bf16[8,1,128,512]{3,2,1,0:T(8,128)(2,1)S(1)} async-done(((bf16[8,1,128,512]{3,2,1,0:T(8,128)(2,1)}), bf16[8,1,128,512]{3,2,1,0:T(8,128)(2,1)S(1)}, u32[]{:S(2)}, u32[]{:S(2)}) %all-to-all-start) | async-done | bytes 1048608 | tf_op jit(solution)/shard_map/all_to_all | solution.py:36
  34.0 1.6 %convert_bitcast_fusion = f32[1,128,8,512]{3,1,0,2:T(8,128)} fusion(bf16[8,1,128,512]{3,2,1,0:T(8,128)(2,1)S(1)} %all-to-all-done), kind=kLoop, calls=%fused_computation.10 | loop fusion | flops 524288 | bytes 3145728 | tf_op jit(solution)/shard_map/convert_element_type | solution.py:22
  35.6 0.0 copy-start.1
  35.6 1.9 %copy.13 = f32[1,128,8,512]{1,3,2,0:T(8,128)S(1)} copy(f32[1,128,8,512]{3,1,0,2:T(8,128)} %convert_bitcast_fusion) | data formatting | bytes 4194304 | tf_op jit(solution)/shard_map/convert_element_type | solution.py:22
  37.5 0.0 copy-done.1
  37.6 2.2 %fusion = (f32[4096]{0:T(1024)S(1)}, f32[128]{0:T(128)S(1)}) fusion(f32[1,128,8,512]{1,3,2,0:T(8,128)S(1)} %copy.13, bf16[128,4096]{0,1:T(8,128)(2,1)S(1)} %copy.11, f32[128]{0:T(128)S(1)} %get-tuple-element.9, s32[4096]{0:T(1024)S(1)} %shift_right_arithmetic.23, s32[128,128]{0,1:T(8,128)S(1)} %copy.12, f32[4096]{0:T(1024)S(1)} %copy-done.1), kind=kLoop, calls=%fused_computation.2 | loop fusion | flops 5762944 | bytes 3261440 | tf_op jit(solution)/shard_map/reduce_sum | solution.py:26
  39.8 2.6 %fusion.6 = bf16[128,4096]{0,1:T(8,128)(2,1)} fusion(bf16[128,4096]{0,1:T(8,128)(2,1)S(1)} %copy.11, f32[1,128,8,512]{1,3,2,0:T(8,128)S(1)} %copy.13, f32[128]{0:T(128)S(1)} %broadcast_multiply_fusion.2, f32[128]{0:T(128)S(1)} %get-tuple-element.9, f32[4096]{0:T(1024)S(1)} %copy-done.1, f32[128]{0:T(128)S(1)} %get-tuple-element.8, ...), kind=kLoop, calls=%fused_computation.9 | loop fusion | flops 6815744 | bytes 4294144 | tf_op jit(solution)/shard_map/convert_element_type | solution.py:25
  42.4 2.3 %copy.14 = bf16[128,4096]{1,0:T(8,128)(2,1)} copy(bf16[128,4096]{0,1:T(8,128)(2,1)} %fusion.6) | data formatting | bytes 2097152
  44.6 22.3 %all-reduce = f32[4096]{0:T(1024)S(1)} all-reduce(f32[4096]{0:T(1024)S(1)} %get-tuple-element.6), channel_id=2, replica_groups=mesh['aa'=4,'ba'=8] {'ba'}, use_global_device_ids=true, to_apply=%region_3.0.clone | all-reduce | flops 4096 | bytes 32768
  66.9 0.1 dynamic-slice.1
  67.0 11.9 %psum.7 = f32[512]{0:T(512)S(1)} all-reduce(f32[512]{0:T(512)S(1)} %dynamic-slice.1), channel_id=1, replica_groups=mesh['aa'=4,'ba'=8] {'aa'}, use_global_device_ids=true, to_apply=%region_4.0 | all-reduce | flops 512 | bytes 4096 | tf_op jit(solution)/shard_map/psum | solution.py:42
  78.9 0.6 broadcast_multiply_fusion
  (3 shorter events, 0.0 us)
Async XLA Ops:
  0.6 18.0 %copy-start = (bf16[128,4096]{1,0:T(8,128)(2,1)S(1)}, bf16[128,4096]{1,0:T(8,128)(2,1)}, u32[]{:S(2)}) copy-start(bf16[128,4096]{1,0:T(8,128)(2,1)} %param.5) | copy-start | bytes 3145732
  13.3 6.1 %copy-start.2 = (s32[128,128]{1,0:T(8,128)S(1)}, s32[128,128]{1,0:T(8,128)}, u32[]{:S(2)}) copy-start(s32[128,128]{1,0:T(8,128)} %param.6) | copy-start | bytes 196612
  13.3 6.2 %copy-start.3 = (u32[32]{0:T(128)S(1)}, u32[32]{0:T(128)}, u32[]{:S(2)}) copy-start(u32[32]{0:T(128)} %constant.16) | copy-start | bytes 388
  13.3 20.7 %all-to-all-start = ((bf16[8,1,128,512]{3,2,1,0:T(8,128)(2,1)}), bf16[8,1,128,512]{3,2,1,0:T(8,128)(2,1)S(1)}, u32[]{:S(2)}, u32[]{:S(2)}) async-start(bf16[8,1,128,512]{3,2,1,0:T(8,128)(2,1)} %bitcast_dynamic-update-slice_fusion), calls=%async_computation | async-start | bytes 2097152 | tf_op jit(solution)/shard_map/all_to_all | solution.py:36
  35.6 1.9 %copy-start.1 = (f32[4096]{0:T(1024)S(1)}, f32[4096]{0:T(1024)}, u32[]{:S(2)}) copy-start(f32[4096]{0:T(1024)} %param.7) | copy-start | bytes 49156
